TPU v7x, 32 devices: a whole 2x2x4 slice. The times are simulated.
32 devices in a mesh: site: 8 (over z, x), dom: 4 (over y, core).
Axes of the slice: x: 2, y: 2, z: 4, core: 2. Of those that a mesh axis runs over, the one named last changes fastest.
Arguments:
- top_partial: float32 [16, 61, 4, 8192], P(None, None, 'dom', 'site'), may hold values from 0.001 to 1
- bottom_partial: float32 [16, 61, 4, 8192], P(None, None, 'dom', 'site'), may hold values from 0.001 to 1
- left_vectors: float32 [256, 61, 61], P('dom'), may hold values from 0.05 to 1
- right_vectors: float32 [256, 61, 61], P('dom'), may hold values from 0.05 to 1
- decay_rates: float32 [256, 61], P('dom'), may hold values from 0.05 to 8
- state_weights: float32 [256, 61], P('dom'), may hold values from 0.002 to 0.05
- part_rates: float32 [256], P('dom'), may hold values from 0.3 to 3
- branch_lengths: float32 [1997], replicated, may hold values from 0.02 to 0.5
- pattern_weights: int32 [4, 8192], P('dom', 'site'), may hold values from 0 to 9
- block_partition: int32 [4, 64], P('dom', 'site'), may hold values from 0 to 255
- chosen_branches: int32 [16], replicated, may hold values from 0 to 1996, as said below
Outputs:
- site_loglik: float32 [16, 4, 8192], P(None, 'dom', 'site')
- part_derivs: float32 [2, 16, 256], P(None, None, 'dom')
- new_lengths: float32 [1997], replicated
Inputs may be any that keep to these rules, and one draw needn't show every extreme that they name: `chosen_branches`: distinct branch numbers.
All inputs are finite; a program needn't handle non-finite values.
Results may differ from a plain program's by a relative error of at most 0.0003.
Values sent between devices are 32-bit elements; how exact they have to be, the bound alone decides.
A program may use at most 64 MiB of HBM per device.

v0:
```python
import jax
import jax.numpy as jnp
from jax import lax
from jax.sharding import PartitionSpec as P

BLK = 128


def project(upper, lower, vec_left, vec_right, state_w):
    scaled = upper * jnp.transpose(state_w)[None, :, :, None]
    lefts = jnp.einsum("binl,nik->bknl", scaled, vec_left, precision=lax.Precision.HIGHEST)
    rights = jnp.einsum("nkj,bjnl->bknl", vec_right, lower, precision=lax.Precision.HIGHEST)
    return (lefts, rights)


def finish(lefts, rights, exponent, times, weight_f):
    joint = lefts * rights
    expo = jnp.transpose(exponent)[None, :, :, None]
    decayed = joint * jnp.exp(expo * times[:, None, None, None])
    like_zero = jnp.sum(decayed, axis=1)
    like_one = jnp.sum(decayed * expo, axis=1)
    like_two = jnp.sum(decayed * expo * expo, axis=1)
    first = like_one / like_zero
    second = like_two / like_zero - first * first
    loglik = weight_f[None] * jnp.log(like_zero)
    sums = jnp.stack(
        [jnp.sum(weight_f[None] * first, axis=-1), jnp.sum(weight_f[None] * second, axis=-1)]
    )
    return (loglik, sums)


def on_device(
    top_partial,
    bottom_partial,
    left_vectors,
    right_vectors,
    decay_rates,
    state_weights,
    part_rates,
    branch_lengths,
    pattern_weights,
    block_partition,
    chosen_branches,
):
    times = branch_lengths[chosen_branches]
    branches = top_partial.shape[0]
    states = top_partial.shape[1]
    sites_here = top_partial.shape[3]
    nblocks = sites_here // BLK
    upper = top_partial.reshape(branches, states, nblocks, BLK)
    lower = bottom_partial.reshape(branches, states, nblocks, BLK)
    blocks = block_partition[0]
    owned = left_vectors.shape[0]
    groups = lax.axis_size("dom")
    parts_all = owned * groups
    wanted = lax.all_gather(block_partition, "dom", axis=0, tiled=True)
    relative = wanted - lax.axis_index("dom") * owned
    inside = jnp.logical_and(relative >= 0, relative < owned).astype(jnp.float32)
    clipped = jnp.clip(relative, 0, owned - 1)
    send_left = left_vectors[clipped] * inside[:, :, None, None]
    send_right = right_vectors[clipped] * inside[:, :, None, None]
    send_decay = decay_rates[clipped] * inside[:, :, None]
    send_weight = state_weights[clipped] * inside[:, :, None]
    send_rate = part_rates[clipped] * inside
    received = (
        lax.all_to_all(send_left, "dom", split_axis=0, concat_axis=0, tiled=True),
        lax.all_to_all(send_right, "dom", split_axis=0, concat_axis=0, tiled=True),
        lax.all_to_all(send_decay, "dom", split_axis=0, concat_axis=0, tiled=True),
        lax.all_to_all(send_weight, "dom", split_axis=0, concat_axis=0, tiled=True),
        lax.all_to_all(send_rate, "dom", split_axis=0, concat_axis=0, tiled=True),
    )
    vec_left = jnp.sum(received[0], axis=0)
    vec_right = jnp.sum(received[1], axis=0)
    decay_b = jnp.sum(received[2], axis=0)
    weight_b = jnp.sum(received[3], axis=0)
    rate_b = jnp.sum(received[4], axis=0)
    exponent = -decay_b * rate_b[:, None]
    lefts, rights = project(upper, lower, vec_left, vec_right, weight_b)
    weight_f = pattern_weights[0].astype(jnp.float32).reshape(nblocks, BLK)
    loglik, sums = finish(lefts, rights, exponent, times, weight_f)
    onehot = (blocks[:, None] == jnp.arange(parts_all, dtype=jnp.int32)[None, :]).astype(
        jnp.float32
    )
    part_local = jnp.einsum("abn,np->abp", sums, onehot, precision=lax.Precision.HIGHEST)
    everything = lax.psum(part_local, ("site", "dom"))
    share = lax.dynamic_slice_in_dim(everything, lax.axis_index("dom") * owned, owned, 2)
    totals = jnp.sum(everything, axis=2)
    updated = times - totals[0] / totals[1]
    new_lengths = branch_lengths.at[chosen_branches].set(updated)
    return (loglik.reshape(branches, 1, sites_here), share, new_lengths)


def solution(mesh):
    return jax.shard_map(
        on_device,
        mesh=mesh,
        in_specs=(
            P(None, None, "dom", "site"),
            P(None, None, "dom", "site"),
            P("dom", None, None),
            P("dom", None, None),
            P("dom", None),
            P("dom", None),
            P("dom"),
            P(),
            P("dom", "site"),
            P("dom", "site"),
            P(),
        ),
        out_specs=(P(None, "dom", "site"), P(None, None, "dom"), P()),
        check_vma=False,
    )
```

profile of v0, /device:TPU:0, one launch (start us, length us, event | category | flops | bytes accessed | tf_op | source)
XLA Modules:
  0.0 121.8 jit_solution(4191838396032848199)
XLA Ops:
  0.6 0.0 copy-start
  0.6 0.8 copy.76
  1.5 6.2 %all-gather = s32[4,1,8]{2,1,0:T(1,128)S(1)} all-gather(s32[1,1,8]{2,1,0:T(1,128)} %bitcast.55), channel_id=1, replica_groups=mesh['site'=8,'dom'=4] {'dom'}, dimensions={0}, use_global_device_ids=true | all-gather | bytes 160 | tf_op jit(solution)/shard_map/all_gather | solution.py:56
  7.7 0.1 reshape.73
  7.8 1.4 %gather_fusion.4 = f32[32]{0:T(128)S(1)} fusion(f32[64]{0:T(128)} %param.17, s32[1024]{0:T(1024)S(1)} %pad_clamp_fusion.1), kind=kCustom, calls=%fused_computation.4 | custom fusion | bytes 384 | tf_op jit(solution)/shard_map/gather | solution.py:64
  9.2 0.1 reshape.104
  9.3 0.6 bitcast_select_fusion
  9.9 3.2 %all-to-all-start.4 = ((f32[4,1,8]{2,1,0:T(1,128)}), f32[4,1,8]{2,1,0:T(1,128)S(1)}, u32[]{:S(2)}, u32[]{:S(2)}) async-start(f32[4,1,8]{2,1,0:T(1,128)} %bitcast.14), calls=%async_computation.4 | async-start | bytes 4096 | tf_op jit(solution)/shard_map/all_to_all | solution.py:70
  13.1 1.3 %gather_fusion.3 = f32[32,61]{1,0:T(8,128)S(1)} fusion(f32[64,61]{1,0:T(8,128)} %param.15, s32[1024]{0:T(1024)S(1)} %pad_clamp_fusion.1), kind=kCustom, calls=%fused_computation.3 | custom fusion | bytes 15744 | tf_op jit(solution)/shard_map/gather | solution.py:62
  14.4 1.3 %gather_fusion.1 = f32[32,61]{1,0:T(8,128)S(1)} fusion(f32[64,61]{1,0:T(8,128)} %param.16, s32[1024]{0:T(1024)S(1)} %pad_clamp_fusion.1), kind=kCustom, calls=%fused_computation.1 | custom fusion | bytes 15744 | tf_op jit(solution)/shard_map/gather | solution.py:63
  15.8 0.1 bitcast_multiply_fusion.2
  15.8 0.7 reshape.156
  16.5 0.3 all-to-all-done.4
  16.8 3.2 %all-to-all-start.3 = ((f32[4,1,488]{2,1,0:T(1,128)}), f32[4,1,488]{2,1,0:T(1,128)S(1)}, u32[]{:S(2)}, u32[]{:S(2)}) async-start(f32[4,1,488]{2,1,0:T(1,128)} %reshape.156), calls=%async_computation.3 | async-start | bytes 16384 | tf_op jit(solution)/shard_map/all_to_all | solution.py:68
  20.1 0.7 reshape.158
  20.7 0.0 copy-done
  20.7 2.7 %gather_fusion.2 = f32[32,61,61]{2,0,1:T(8,128)S(1)} fusion(f32[64,61,61]{2,0,1:T(8,128)S(1)} %copy-done, s32[1024]{0:T(1024)S(1)} %pad_clamp_fusion.1), kind=kCustom, calls=%fused_computation.2 | custom fusion | bytes 952704 | tf_op jit(solution)/shard_map/gather | solution.py:61
  23.5 5.3 %gather_fusion = f32[32,61,61]{2,0,1:T(8,128)} fusion(f32[64,61,61]{2,0,1:T(8,128)} %param.13, s32[1024]{0:T(1024)S(1)} %pad_clamp_fusion.1), kind=kCustom, calls=%fused_computation | custom fusion | bytes 952704 | tf_op jit(solution)/shard_map/gather | solution.py:60
  28.8 0.0 all-to-all-done.3
  28.8 3.4 %all-to-all-start.1 = ((f32[4,1,488]{2,1,0:T(1,128)}), f32[4,1,488]{2,1,0:T(1,128)S(1)}, u32[]{:S(2)}, u32[]{:S(2)}) async-start(f32[4,1,488]{2,1,0:T(1,128)} %reshape.158), calls=%async_computation.1 | async-start | bytes 16384 | tf_op jit(solution)/shard_map/all_to_all | solution.py:69
  32.2 2.8 %copy_multiply_fusion.5 = (f32[4,8,61,61]{3,1,2,0:T(8,128)}, f32[4,8,61,61]{3,1,2,0:T(8,128)}) fusion(f32[4,8]{1,0:T(4,128)S(1)} %bitcast_convert_fusion, f32[32,61,61]{2,0,1:T(8,128)S(1)} %gather_fusion.2, f32[32,61,61]{2,0,1:T(8,128)} %gather_fusion), kind=kLoop, calls=%fused_computation.16 | loop fusion | flops 238144 | bytes 1905280 | tf_op jit(solution)/shard_map/mul | solution.py:60
  35.0 3.2 %reshape.160 = f32[4,1,29768]{2,1,0:T(1,128)} reshape(f32[4,61,8,61]{3,2,1,0:T(8,128)} %bitcast.46) | data formatting | bytes 952576
  38.2 0.0 all-to-all-done.1
  38.2 3.5 %all-to-all-start = ((f32[4,1,29768]{2,1,0:T(1,128)}), f32[4,1,29768]{2,1,0:T(1,128)S(1)}, u32[]{:S(2)}, u32[]{:S(2)}) async-start(f32[4,1,29768]{2,1,0:T(1,128)} %reshape.160), calls=%async_computation | async-start | bytes 954368 | tf_op jit(solution)/shard_map/all_to_all | solution.py:66
  41.6 0.0 copy-done.13
  41.7 0.0 copy-start.9
  41.7 0.0 copy-done.7
  41.7 3.1 %reshape.154 = f32[4,1,29768]{2,1,0:T(1,128)} reshape(f32[4,61,8,61]{3,2,1,0:T(8,128)} %bitcast.45) | data formatting | bytes 952576
  44.8 0.0 copy-done.9
  44.8 0.7 gather_fusion.5
  45.5 0.5 broadcast.86
  46.0 0.7 reduce.1
  46.7 0.1 reshape.157
  46.8 0.7 reduce.3
  47.5 0.1 reshape.159
  47.6 0.6 reduce_sum.100
  48.2 0.1 multiply_bitcast_fusion
  48.3 1.7 %all-to-all-done = f32[4,1,29768]{2,1,0:T(1,128)S(1)} async-done(((f32[4,1,29768]{2,1,0:T(1,128)}), f32[4,1,29768]{2,1,0:T(1,128)S(1)}, u32[]{:S(2)}, u32[]{:S(2)}) %all-to-all-start) | async-done | bytes 476320 | tf_op jit(solution)/shard_map/all_to_all | solution.py:66
  49.9 4.3 %all-to-all-start.2 = ((f32[4,1,29768]{2,1,0:T(1,128)}), f32[4,1,29768]{2,1,0:T(1,128)}, u32[]{:S(2)}, u32[]{:S(2)}) async-start(f32[4,1,29768]{2,1,0:T(1,128)} %reshape.154), calls=%async_computation.2 | async-start | bytes 954368 | tf_op jit(solution)/shard_map/all_to_all | solution.py:67
  54.2 0.1 multiply_exponential_fusion
  54.3 2.1 %reduce.4 = f32[4,29768]{1,0:T(4,128)S(1)} reduce(f32[4,1,29768]{2,1,0:T(1,128)S(1)} %all-to-all-done, f32[]{:T(128)} %broadcast.86), dimensions={1}, to_apply=%all_to_all.18.reduce_sub_computation | reduce | bytes 952580 | tf_op jit(solution)/shard_map/all_to_all | solution.py:66
  56.4 0.6 reshape.161
  57.0 0.8 bitcast_reduce_fusion
  57.7 4.7 %all-to-all-done.2 = f32[4,1,29768]{2,1,0:T(1,128)} async-done(((f32[4,1,29768]{2,1,0:T(1,128)}), f32[4,1,29768]{2,1,0:T(1,128)}, u32[]{:S(2)}, u32[]{:S(2)}) %all-to-all-start.2) | async-done | bytes 476320 | tf_op jit(solution)/shard_map/all_to_all | solution.py:67
  62.4 2.9 %reduce.2 = f32[4,29768]{1,0:T(4,128)S(1)} reduce(f32[4,1,29768]{2,1,0:T(1,128)} %all-to-all-done.2, f32[]{:T(128)} %broadcast.86), dimensions={1}, to_apply=%all_to_all.20.reduce_sub_computation | reduce | bytes 952580 | tf_op jit(solution)/shard_map/all_to_all | solution.py:67
  65.3 0.6 reshape.155
  65.9 0.1 bitcast_reduce_fusion.1
  66.0 0.0 copy-start.2
  66.0 0.0 copy-start.4
  66.0 0.0 copy-start.8
  66.0 0.0 copy-start.12
  66.0 6.8 %fusion = f32[8,61,16,128]{3,1,2,0:T(8,128)S(1)} fusion(f32[16,61,8,128]{3,2,1,0:T(8,128)} %bitcast.44, f32[8,61,61,1]{2,0,1,3:T(8,128)S(1)} %bitcast.47), kind=kOutput, calls=%fused_computation.8 | convolution fusion | flops 731578368 | bytes 8114464 | tf_op jit(solution)/shard_map/nkj,bjnl->bknl/dot_general | solution.py:12
  72.9 0.0 copy-start.11
  72.9 6.4 %multiply_reduce_fusion.1 = (f32[16,8,128]{2,0,1:T(8,128)S(1)}, f32[16,8,128]{2,0,1:T(8,128)S(1)}, f32[16,8,128]{2,0,1:T(8,128)S(1)}) fusion(f32[61,8]{0,1:T(8,128)S(1)} %copy-done.4, f32[16,61,8]{1,0,2:T(8,128)S(1)} %multiply_exponential_fusion, f32[8,61,16,128]{3,1,2,0:T(8,128)S(1)} %fusion, f32[16,61,8,128]{3,2,1,0:T(8,128)S(1)} %bitcast.57, ...), kind=kOutput, calls=%fused_computation.13 | convolution fusion | flops 739524608 | bytes 8346208 | tf_op jit(solution)/shard_map/binl,nik->bknl/dot_general | solution.py:11
  79.3 0.1 multiply_reduce_fusion.3
  79.5 0.0 copy-done.11
  79.5 0.2 fusion.6
  79.7 39.9 %psum.7 = f32[2,16,256]{2,1,0:T(8,128)S(1)} all-reduce(f32[2,16,256]{2,1,0:T(8,128)S(1)} %fusion.6), channel_id=1, replica_groups=mesh['site'=8,'dom'=4] {'site','dom'}, use_global_device_ids=true, to_apply=%region_10.11 | all-reduce | flops 8192 | bytes 65536 | tf_op jit(solution)/shard_map/psum | solution.py:85
  119.6 0.1 reduce_sum.109
  119.7 0.7 constant_dynamic-slice_fusion
  120.4 0.0 copy-done.10
  120.4 0.6 scatter_fusion
  121.0 0.0 copy-start.1
  121.1 0.7 copy.45
  (28 shorter events, 0.2 us)
Async XLA Ops:
  0.6 20.1 %copy-start = (f32[64,61,61]{2,0,1:T(8,128)S(1)}, f32[64,61,61]{2,0,1:T(8,128)}, u32[]{:S(2)}) copy-start(f32[64,61,61]{2,0,1:T(8,128)} %param.14) | copy-start | bytes 2857732
  9.9 6.9 %all-to-all-start.4 = ((f32[4,1,8]{2,1,0:T(1,128)}), f32[4,1,8]{2,1,0:T(1,128)S(1)}, u32[]{:S(2)}, u32[]{:S(2)}) async-start(f32[4,1,8]{2,1,0:T(1,128)} %bitcast.14), calls=%async_computation.4 | async-start | bytes 4096 | tf_op jit(solution)/shard_map/all_to_all | solution.py:70
  16.8 12.0 %all-to-all-start.3 = ((f32[4,1,488]{2,1,0:T(1,128)}), f32[4,1,488]{2,1,0:T(1,128)S(1)}, u32[]{:S(2)}, u32[]{:S(2)}) async-start(f32[4,1,488]{2,1,0:T(1,128)} %reshape.156), calls=%async_computation.3 | async-start | bytes 16384 | tf_op jit(solution)/shard_map/all_to_all | solution.py:68
  28.8 12.9 %copy-start.13 = (s32[16]{0:T(128)S(1)}, s32[16]{0:T(128)}, u32[]{:S(2)}) copy-start(s32[16]{0:T(128)} %param.21) | copy-start | bytes 196
  28.8 12.9 %copy-start.7 = (s32[1,1024]{1,0:T(1,128)S(1)}, s32[1,1024]{1,0:T(1,128)}, u32[]{:S(2)}) copy-start(s32[1,1024]{1,0:T(1,128)} %param.19) | copy-start | bytes 12292
  28.8 9.4 %all-to-all-start.1 = ((f32[4,1,488]{2,1,0:T(1,128)}), f32[4,1,488]{2,1,0:T(1,128)S(1)}, u32[]{:S(2)}, u32[]{:S(2)}) async-start(f32[4,1,488]{2,1,0:T(1,128)} %reshape.158), calls=%async_computation.1 | async-start | bytes 16384 | tf_op jit(solution)/shard_map/all_to_all | solution.py:69
  38.2 11.8 %all-to-all-start = ((f32[4,1,29768]{2,1,0:T(1,128)}), f32[4,1,29768]{2,1,0:T(1,128)S(1)}, u32[]{:S(2)}, u32[]{:S(2)}) async-start(f32[4,1,29768]{2,1,0:T(1,128)} %reshape.160), calls=%async_computation | async-start | bytes 954368 | tf_op jit(solution)/shard_map/all_to_all | solution.py:66
  41.7 3.2 %copy-start.9 = (s32[16]{0:T(128)}, s32[16]{0:T(128)S(1)}, u32[]{:S(2)}) copy-start(s32[16]{0:T(128)S(1)} %compare_select_fusion.1) | copy-start | bytes 196
  45.5 8.7 %copy-start.5 = (f32[16]{0:T(128)}, f32[16]{0:T(128)S(1)}, u32[]{:S(2)}) copy-start(f32[16]{0:T(128)S(1)} %gather_fusion.5) | copy-start | bytes 196
  48.2 6.1 %copy-start.3 = (f32[61,8]{0,1:T(8,128)}, f32[61,8]{0,1:T(8,128)S(1)}, u32[]{:S(2)}) copy-start(f32[61,8]{0,1:T(8,128)S(1)} %multiply_bitcast_fusion) | copy-start | bytes 5860
  49.9 12.5 %all-to-all-start.2 = ((f32[4,1,29768]{2,1,0:T(1,128)}), f32[4,1,29768]{2,1,0:T(1,128)}, u32[]{:S(2)}, u32[]{:S(2)}) async-start(f32[4,1,29768]{2,1,0:T(1,128)} %reshape.154), calls=%async_computation.2 | async-start | bytes 954368 | tf_op jit(solution)/shard_map/all_to_all | solution.py:67
  66.0 6.9 %copy-start.2 = (f32[8,61,61]{2,0,1:T(8,128)S(1)}, f32[8,61,61]{2,0,1:T(8,128)}, u32[]{:S(2)}) copy-start(f32[8,61,61]{2,0,1:T(8,128)} %bitcast_reduce_fusion) | copy-start | bytes 357220
  66.0 6.9 %copy-start.4 = (f32[61,8]{0,1:T(8,128)S(1)}, f32[61,8]{0,1:T(8,128)}, u32[]{:S(2)}) copy-start(f32[61,8]{0,1:T(8,128)} %copy-done.3) | copy-start | bytes 5860
  66.0 6.9 %copy-start.8 = (f32[8,61]{1,0:T(8,128)S(1)}, f32[8,61]{1,0:T(8,128)}, u32[]{:S(2)}) copy-start(f32[8,61]{1,0:T(8,128)} %reduce_sum.100) | copy-start | bytes 5860
  66.0 6.9 %copy-start.12 = (f32[16,61,1,1024]{3,2,1,0:T(1,128)S(1)}, f32[16,61,1,1024]{3,2,1,0:T(1,128)}, u32[]{:S(2)}) copy-start(f32[16,61,1,1024]{3,2,1,0:T(1,128)} %param.11) | copy-start | bytes 11993092
  72.9 6.6 %copy-start.11 = (s32[1,8]{1,0:T(1,128)S(1)}, s32[1,8]{1,0:T(1,128)}, u32[]{:S(2)}) copy-start(s32[1,8]{1,0:T(1,128)} %param.20) | copy-start | bytes 100
  72.9 47.5 %copy-start.6 = (f32[16]{0:T(128)S(1)}, f32[16]{0:T(128)}, u32[]{:S(2)}) copy-start(f32[16]{0:T(128)} %copy-done.5) | copy-start | bytes 196
  72.9 47.5 %copy-start.10 = (s32[16]{0:T(128)S(1)}, s32[16]{0:T(128)}, u32[]{:S(2)}) copy-start(s32[16]{0:T(128)} %copy-done.9) | copy-start | bytes 196
  121.0 0.8 copy-start.1
where the time goes:
time: 123 us; the launch traced here: 122 us
  blocking collectives  46.1 us (37%)
  local copies, waits for them, and re-layouts  25.3 us (21%)
  starting transfers between devices  17.6 us (14%)
  matrix products  13.5 us (11%)
  other arithmetic  11.7 us (10%)
  waiting for transfers between devices  6.6 us (5%)
    psum x1, blocking collectives, on_device(): everything = lax.psum(part_local, ('site', 'dom'))  39.9 us
    unnamed x38, local copies, waits for them, and re-layouts  10.6 us
    dot_general x1, matrix products, project(): jnp.einsum('nkj,bjnl->bknl', vec_right, lower, precision=lax.Precision.HI...  6.82 us
    dot_general x1, matrix products, project(): jnp.einsum('binl,nik->bknl', scaled, vec_left, precision=lax.Precision.HI...  6.42 us
    all_gather x1, blocking collectives, on_device(): wanted = lax.all_gather(block_partition, 'dom', axis=0, tiled=True)  6.22 us
    gather x1, local copies, waits for them, and re-layouts, on_device(): send_left = left_vectors[clipped] * inside[:, :, None, None]  5.29 us
    all_to_all x1, waiting for transfers between devices, on_device(): lax.all_to_all(send_right, 'dom', split_axis=0, concat_axis=0, tiled=True)  4.67 us
    all_to_all x1, starting transfers between devices, on_device(): lax.all_to_all(send_right, 'dom', split_axis=0, concat_axis=0, tiled=True)  4.3 us
  transfers between devices with their start and end apart: 5, of which 3 were waited for; matrix products, arithmetic and copies ran while one was open for 23% of the time, Pallas kernels for 0%

commit v1 on v0

--- a/solution.py
+++ b/solution.py
@@ -2,6 +2,7 @@
 import jax.numpy as jnp
 from jax import lax
 from jax.sharding import PartitionSpec as P
+from jax.lax import all_gather
 
 BLK = 128
 
@@ -82,7 +83,7 @@
         jnp.float32
     )
     part_local = jnp.einsum("abn,np->abp", sums, onehot, precision=lax.Precision.HIGHEST)
-    everything = lax.psum(part_local, ("site", "dom"))
+    everything = jnp.sum(all_gather(part_local, axis_name=("site", "dom")), axis=0)
     share = lax.dynamic_slice_in_dim(everything, lax.axis_index("dom") * owned, owned, 2)
     totals = jnp.sum(everything, axis=2)
     updated = times - totals[0] / totals[1]

time: 123 us -> 153 us (1.24)
  waiting for transfers between devices: 6.6 us -> 60.2 us
  blocking collectives: 46.1 us -> 6.22 us
  between operations: 0.99 us -> 14.4 us
  other arithmetic: 11.7 us -> 14.4 us
    all_gather x0 -> x1, waiting for transfers between devices: none -> 53.6 us  [on_device(): all_gather(part_local, axis_name=('site', 'dom'))]
    psum x1 -> x0, blocking collectives: 39.9 us -> none  [on_device(): everything = lax.psum(part_local, ('site', 'dom'))]
  transfers between devices with their start and end apart: 5 -> 6, of which waited for: 3 -> 4; matrix products, arithmetic and copies ran while one was open for 23% -> 19% of each run, Pallas kernels for 0% -> 0%
where the time goes in v1:
time: 153 us; the launch traced here: 152 us
  waiting for transfers between devices  60.2 us (39%)
  local copies, waits for them, and re-layouts  25.3 us (17%)
  starting transfers between devices  17.7 us (12%)
  other arithmetic  14.4 us (9%)
  between operations  14.4 us (9%)
  matrix products  14.1 us (9%)
  blocking collectives  6.22 us (4%)
    all_gather x1, waiting for transfers between devices, on_device(): all_gather(part_local, axis_name=('site', 'dom'))  53.6 us
    unnamed x38, local copies, waits for them, and re-layouts  10.6 us
    dot_general x1, matrix products, project(): jnp.einsum('nkj,bjnl->bknl', vec_right, lower, precision=lax.Precision.HI...  6.82 us
    dot_general x1, matrix products, project(): jnp.einsum('binl,nik->bknl', scaled, vec_left, precision=lax.Precision.HI...  6.42 us
    all_gather x1, blocking collectives, on_device(): wanted = lax.all_gather(block_partition, 'dom', axis=0, tiled=True)  6.22 us
    gather x1, local copies, waits for them, and re-layouts, on_device(): send_left = left_vectors[clipped] * inside[:, :, None, None]  5.29 us
    all_to_all x1, waiting for transfers between devices, on_device(): lax.all_to_all(send_right, 'dom', split_axis=0, concat_axis=0, tiled=True)  4.62 us
    all_to_all x1, starting transfers between devices, on_device(): lax.all_to_all(send_right, 'dom', split_axis=0, concat_axis=0, tiled=True)  4.12 us
  transfers between devices with their start and end apart: 6, of which 4 were waited for; matrix products, arithmetic and copies ran while one was open for 19% of the time, Pallas kernels for 0%

profile of v1, /device:TPU:0, one launch (start us, length us, event | category | flops | bytes accessed | tf_op | source)
XLA Modules:
  0.0 152.3 jit_solution(3823639845382890914)
XLA Ops:
  7.2 0.0 copy-start
  7.2 0.8 copy.110
  8.0 6.2 %all-gather.1 = s32[4,1,8]{2,1,0:T(1,128)S(1)} all-gather(s32[1,1,8]{2,1,0:T(1,128)} %bitcast.59), channel_id=1, replica_groups=mesh['site'=8,'dom'=4] {'dom'}, dimensions={0}, use_global_device_ids=true | all-gather | bytes 160 | tf_op jit(solution)/shard_map/all_gather | solution.py:57
  14.3 0.1 reshape.73
  14.4 1.4 gather_fusion.4
  15.7 0.1 reshape.104
  15.8 0.6 bitcast_select_fusion
  16.4 3.2 %all-to-all-start.4 = ((f32[4,1,8]{2,1,0:T(1,128)}), f32[4,1,8]{2,1,0:T(1,128)S(1)}, u32[]{:S(2)}, u32[]{:S(2)}) async-start(f32[4,1,8]{2,1,0:T(1,128)} %bitcast.14), calls=%async_computation.4 | async-start | bytes 4096 | tf_op jit(solution)/shard_map/all_to_all | solution.py:71
  19.6 1.3 gather_fusion.3
  21.0 1.3 gather_fusion.1
  22.3 0.1 bitcast_multiply_fusion.2
  22.4 0.7 reshape.158
  23.1 0.3 all-to-all-done.4
  23.3 3.2 %all-to-all-start.3 = ((f32[4,1,488]{2,1,0:T(1,128)}), f32[4,1,488]{2,1,0:T(1,128)S(1)}, u32[]{:S(2)}, u32[]{:S(2)}) async-start(f32[4,1,488]{2,1,0:T(1,128)} %reshape.158), calls=%async_computation.3 | async-start | bytes 16384 | tf_op jit(solution)/shard_map/all_to_all | solution.py:69
  26.6 0.7 reshape.160
  27.3 0.0 copy-done
  27.3 2.7 %gather_fusion.2 = f32[32,61,61]{2,0,1:T(8,128)S(1)} fusion(f32[64,61,61]{2,0,1:T(8,128)S(1)} %copy-done, s32[1024]{0:T(1024)S(1)} %pad_clamp_fusion.1), kind=kCustom, calls=%fused_computation.2 | custom fusion | bytes 952704 | tf_op jit(solution)/shard_map/gather | solution.py:62
  30.0 5.3 %gather_fusion = f32[32,61,61]{2,0,1:T(8,128)} fusion(f32[64,61,61]{2,0,1:T(8,128)} %param.13, s32[1024]{0:T(1024)S(1)} %pad_clamp_fusion.1), kind=kCustom, calls=%fused_computation | custom fusion | bytes 952704 | tf_op jit(solution)/shard_map/gather | solution.py:61
  35.3 0.0 all-to-all-done.3
  35.3 3.4 %all-to-all-start.1 = ((f32[4,1,488]{2,1,0:T(1,128)}), f32[4,1,488]{2,1,0:T(1,128)S(1)}, u32[]{:S(2)}, u32[]{:S(2)}) async-start(f32[4,1,488]{2,1,0:T(1,128)} %reshape.160), calls=%async_computation.1 | async-start | bytes 16384 | tf_op jit(solution)/shard_map/all_to_all | solution.py:70
  38.7 2.8 %copy_multiply_fusion.5 = (f32[4,8,61,61]{3,1,2,0:T(8,128)}, f32[4,8,61,61]{3,1,2,0:T(8,128)}) fusion(f32[4,8]{1,0:T(4,128)S(1)} %bitcast_convert_fusion, f32[32,61,61]{2,0,1:T(8,128)S(1)} %gather_fusion.2, f32[32,61,61]{2,0,1:T(8,128)} %gather_fusion), kind=kLoop, calls=%fused_computation.16 | loop fusion | flops 238144 | bytes 1905280 | tf_op jit(solution)/shard_map/mul | solution.py:61
  41.5 3.2 %reshape.162 = f32[4,1,29768]{2,1,0:T(1,128)} reshape(f32[4,61,8,61]{3,2,1,0:T(8,128)} %bitcast.49) | data formatting | bytes 952576
  44.7 0.0 all-to-all-done.1
  44.7 3.5 %all-to-all-start = ((f32[4,1,29768]{2,1,0:T(1,128)}), f32[4,1,29768]{2,1,0:T(1,128)S(1)}, u32[]{:S(2)}, u32[]{:S(2)}) async-start(f32[4,1,29768]{2,1,0:T(1,128)} %reshape.162), calls=%async_computation | async-start | bytes 954368 | tf_op jit(solution)/shard_map/all_to_all | solution.py:67
  48.2 0.0 copy-done.13
  48.2 0.0 copy-done.7
  48.2 0.0 copy-start.9
  48.2 3.1 %reshape.156 = f32[4,1,29768]{2,1,0:T(1,128)} reshape(f32[4,61,8,61]{3,2,1,0:T(8,128)} %bitcast.48) | data formatting | bytes 952576
  51.4 0.7 gather_fusion.5
  52.1 0.5 broadcast.86
  52.6 0.7 reduce.4
  53.3 0.1 reshape.159
  53.3 0.7 reduce.6
  54.0 0.1 reshape.161
  54.1 0.6 reduce_sum.109
  54.7 0.1 multiply_bitcast_fusion
  54.8 1.7 %all-to-all-done = f32[4,1,29768]{2,1,0:T(1,128)S(1)} async-done(((f32[4,1,29768]{2,1,0:T(1,128)}), f32[4,1,29768]{2,1,0:T(1,128)S(1)}, u32[]{:S(2)}, u32[]{:S(2)}) %all-to-all-start) | async-done | bytes 476320 | tf_op jit(solution)/shard_map/all_to_all | solution.py:67
  56.4 4.1 %all-to-all-start.2 = ((f32[4,1,29768]{2,1,0:T(1,128)}), f32[4,1,29768]{2,1,0:T(1,128)}, u32[]{:S(2)}, u32[]{:S(2)}) async-start(f32[4,1,29768]{2,1,0:T(1,128)} %reshape.156), calls=%async_computation.2 | async-start | bytes 954368 | tf_op jit(solution)/shard_map/all_to_all | solution.py:68
  60.6 0.2 all-gather.4.cloned.1.call-start
  60.8 0.0 copy-done.5
  60.8 0.1 multiply_exponential_fusion
  60.9 2.1 %reduce.7 = f32[4,29768]{1,0:T(4,128)S(1)} reduce(f32[4,1,29768]{2,1,0:T(1,128)S(1)} %all-to-all-done, f32[]{:T(128)} %broadcast.86), dimensions={1}, to_apply=%all_to_all.18.reduce_sub_computation | reduce | bytes 952580 | tf_op jit(solution)/shard_map/all_to_all | solution.py:67
  63.0 0.6 reshape.163
  63.6 0.8 bitcast_reduce_fusion
  64.3 4.6 %all-to-all-done.2 = f32[4,1,29768]{2,1,0:T(1,128)} async-done(((f32[4,1,29768]{2,1,0:T(1,128)}), f32[4,1,29768]{2,1,0:T(1,128)}, u32[]{:S(2)}, u32[]{:S(2)}) %all-to-all-start.2) | async-done | bytes 476320 | tf_op jit(solution)/shard_map/all_to_all | solution.py:68
  68.9 2.9 %reduce.5 = f32[4,29768]{1,0:T(4,128)S(1)} reduce(f32[4,1,29768]{2,1,0:T(1,128)} %all-to-all-done.2, f32[]{:T(128)} %broadcast.86), dimensions={1}, to_apply=%all_to_all.20.reduce_sub_computation | reduce | bytes 952580 | tf_op jit(solution)/shard_map/all_to_all | solution.py:68
  71.9 0.6 reshape.157
  72.4 0.1 bitcast_reduce_fusion.1
  72.5 0.0 copy-start.4
  72.5 0.0 copy-start.8
  72.5 0.0 copy-start.12
  72.6 6.8 %fusion = f32[8,61,16,128]{3,1,2,0:T(8,128)S(1)} fusion(f32[16,61,8,128]{3,2,1,0:T(8,128)} %bitcast.46, f32[8,61,61,1]{2,0,1,3:T(8,128)S(1)} %bitcast.50), kind=kOutput, calls=%fused_computation.8 | convolution fusion | flops 731578368 | bytes 8114464 | tf_op jit(solution)/shard_map/nkj,bjnl->bknl/dot_general | solution.py:13
  79.4 0.0 copy-start.11
  79.5 6.4 %multiply_reduce_fusion.1 = (f32[16,8,128]{2,0,1:T(8,128)S(1)}, f32[16,8,128]{2,0,1:T(8,128)S(1)}, f32[16,8,128]{2,0,1:T(8,128)S(1)}) fusion(f32[61,8]{0,1:T(8,128)S(1)} %copy-done.4, f32[16,61,8]{1,0,2:T(8,128)S(1)} %multiply_exponential_fusion, f32[8,61,16,128]{3,1,2,0:T(8,128)S(1)} %fusion, f32[16,61,8,128]{3,2,1,0:T(8,128)S(1)} %bitcast.61, ...), kind=kOutput, calls=%fused_computation.13 | convolution fusion | flops 739524608 | bytes 8346208 | tf_op jit(solution)/shard_map/binl,nik->bknl/dot_general | solution.py:12
  85.9 0.1 multiply_reduce_fusion.3
  86.0 0.8 fusion.6
  86.8 0.0 all-gather.4.cloned.1.call-update
  86.9 0.7 copy.76
  87.6 53.6 %all-gather.4.cloned.1.call-done = f32[64,16,256]{2,1,0:T(8,128)} async-done(((f32[2,16,256]{2,1,0:T(8,128)}), f32[64,16,256]{2,1,0:T(8,128)}) %all-gather.4.cloned.1.call-update) | async-done | bytes 1048592 | tf_op jit(solution)/shard_map/all_gather | solution.py:86
  141.3 1.3 reduce_sum.118
  142.6 1.4 reduce.2
  144.1 0.6 scatter_fusion
  144.7 0.0 copy-start.1
  144.7 0.7 constant_dynamic-slice_fusion
  (32 shorter events, 0.2 us)
Async XLA Ops:
  7.2 20.1 %copy-start = (f32[64,61,61]{2,0,1:T(8,128)S(1)}, f32[64,61,61]{2,0,1:T(8,128)}, u32[]{:S(2)}) copy-start(f32[64,61,61]{2,0,1:T(8,128)} %param.14) | copy-start | bytes 2857732
  16.4 6.9 %all-to-all-start.4 = ((f32[4,1,8]{2,1,0:T(1,128)}), f32[4,1,8]{2,1,0:T(1,128)S(1)}, u32[]{:S(2)}, u32[]{:S(2)}) async-start(f32[4,1,8]{2,1,0:T(1,128)} %bitcast.14), calls=%async_computation.4 | async-start | bytes 4096 | tf_op jit(solution)/shard_map/all_to_all | solution.py:71
  23.3 12.0 %all-to-all-start.3 = ((f32[4,1,488]{2,1,0:T(1,128)}), f32[4,1,488]{2,1,0:T(1,128)S(1)}, u32[]{:S(2)}, u32[]{:S(2)}) async-start(f32[4,1,488]{2,1,0:T(1,128)} %reshape.158), calls=%async_computation.3 | async-start | bytes 16384 | tf_op jit(solution)/shard_map/all_to_all | solution.py:69
  35.3 12.9 %copy-start.13 = (s32[16]{0:T(128)S(1)}, s32[16]{0:T(128)}, u32[]{:S(2)}) copy-start(s32[16]{0:T(128)} %param.21) | copy-start | bytes 196
  35.3 12.9 %copy-start.7 = (s32[1,1024]{1,0:T(1,128)S(1)}, s32[1,1024]{1,0:T(1,128)}, u32[]{:S(2)}) copy-start(s32[1,1024]{1,0:T(1,128)} %param.19) | copy-start | bytes 12292
  35.3 9.4 %all-to-all-start.1 = ((f32[4,1,488]{2,1,0:T(1,128)}), f32[4,1,488]{2,1,0:T(1,128)S(1)}, u32[]{:S(2)}, u32[]{:S(2)}) async-start(f32[4,1,488]{2,1,0:T(1,128)} %reshape.160), calls=%async_computation.1 | async-start | bytes 16384 | tf_op jit(solution)/shard_map/all_to_all | solution.py:70
  44.7 11.8 %all-to-all-start = ((f32[4,1,29768]{2,1,0:T(1,128)}), f32[4,1,29768]{2,1,0:T(1,128)S(1)}, u32[]{:S(2)}, u32[]{:S(2)}) async-start(f32[4,1,29768]{2,1,0:T(1,128)} %reshape.162), calls=%async_computation | async-start | bytes 954368 | tf_op jit(solution)/shard_map/all_to_all | solution.py:67
  48.2 3.2 %copy-start.9 = (s32[16]{0:T(128)}, s32[16]{0:T(128)S(1)}, u32[]{:S(2)}) copy-start(s32[16]{0:T(128)S(1)} %compare_select_fusion.1) | copy-start | bytes 196
  52.0 8.8 %copy-start.5 = (f32[16]{0:T(128)}, f32[16]{0:T(128)S(1)}, u32[]{:S(2)}) copy-start(f32[16]{0:T(128)S(1)} %gather_fusion.5) | copy-start | bytes 196
  54.8 6.1 %copy-start.3 = (f32[61,8]{0,1:T(8,128)}, f32[61,8]{0,1:T(8,128)S(1)}, u32[]{:S(2)}) copy-start(f32[61,8]{0,1:T(8,128)S(1)} %multiply_bitcast_fusion) | copy-start | bytes 5860
  56.4 12.5 %all-to-all-start.2 = ((f32[4,1,29768]{2,1,0:T(1,128)}), f32[4,1,29768]{2,1,0:T(1,128)}, u32[]{:S(2)}, u32[]{:S(2)}) async-start(f32[4,1,29768]{2,1,0:T(1,128)} %reshape.156), calls=%async_computation.2 | async-start | bytes 954368 | tf_op jit(solution)/shard_map/all_to_all | solution.py:68
  60.6 80.7 %all-gather.4.cloned.1.call-start = ((), (), s32[]{:S(2)}) async-start(), calls=%async_computation.5 | async-start | bytes 1081344 | tf_op jit(solution)/shard_map/all_gather | solution.py:86
  72.5 6.9 %copy-start.2 = (f32[8,61,61]{2,0,1:T(8,128)S(1)}, f32[8,61,61]{2,0,1:T(8,128)}, u32[]{:S(2)}) copy-start(f32[8,61,61]{2,0,1:T(8,128)} %bitcast_reduce_fusion) | copy-start | bytes 357220
  72.5 6.9 %copy-start.4 = (f32[61,8]{0,1:T(8,128)S(1)}, f32[61,8]{0,1:T(8,128)}, u32[]{:S(2)}) copy-start(f32[61,8]{0,1:T(8,128)} %copy-done.3) | copy-start | bytes 5860
  72.5 6.9 %copy-start.8 = (f32[8,61]{1,0:T(8,128)S(1)}, f32[8,61]{1,0:T(8,128)}, u32[]{:S(2)}) copy-start(f32[8,61]{1,0:T(8,128)} %reduce_sum.109) | copy-start | bytes 5860
  72.5 6.9 %copy-start.12 = (f32[16,61,1,1024]{3,2,1,0:T(1,128)S(1)}, f32[16,61,1,1024]{3,2,1,0:T(1,128)}, u32[]{:S(2)}) copy-start(f32[16,61,1,1024]{3,2,1,0:T(1,128)} %param.11) | copy-start | bytes 11993092
  79.4 6.6 %copy-start.11 = (s32[1,8]{1,0:T(1,128)S(1)}, s32[1,8]{1,0:T(1,128)}, u32[]{:S(2)}) copy-start(s32[1,8]{1,0:T(1,128)} %param.20) | copy-start | bytes 100
  79.4 64.6 %copy-start.6 = (f32[16]{0:T(128)S(1)}, f32[16]{0:T(128)}, u32[]{:S(2)}) copy-start(f32[16]{0:T(128)} %copy-done.5) | copy-start | bytes 196
  79.4 64.6 %copy-start.10 = (s32[16]{0:T(128)S(1)}, s32[16]{0:T(128)}, u32[]{:S(2)}) copy-start(s32[16]{0:T(128)} %copy-done.9) | copy-start | bytes 196
  144.7 0.7 copy-start.1
Sparse Core Ops, SparseCore 0:
  87.0 54.2 all-gather.3
